TPU v7x, 128 devices: a whole 4x4x4 slice. The times are simulated.
128 devices in a mesh: dp: 4 (over x), fsdp: 32 (over z, y, core).
Axes of the slice: x: 4, y: 4, z: 4, core: 2. Of those that a mesh axis runs over, the one named last changes fastest.
Arguments:
- gradient: bfloat16 [4, 4096, 8, 1024], P('dp', 'fsdp'), may hold values from -3 to 3
- block_owner_index: int32 [32], replicated, may hold values from 0 to 31, as said below
- block_grid_cell: int32 [32], replicated, may hold values from 0 to 31, each once
- left_eigen_basis: float32 [64, 1024, 1024], P('fsdp', None, 'dp'), may hold values from -0.1875 to 0.1875
- right_eigen_basis: float32 [64, 1024, 1024], P('fsdp', None, 'dp'), may hold values from -0.1875 to 0.1875
- left_statistic_matrix: float32 [64, 1024, 1024], P('fsdp', None, 'dp'), may hold values from -6 to 6
- right_statistic_matrix: float32 [64, 1024, 1024], P('fsdp', None, 'dp'), may hold values from -6 to 6
- first_adam_moment: float32 [64, 1024, 1024], P('fsdp', None, 'dp'), may hold values from -0.09 to 0.09
- second_adam_moment: float32 [64, 1024, 1024], P('fsdp', None, 'dp'), may hold values from 1e-05 to 0.001
Outputs:
- new_left_stat: float32 [64, 1024, 1024], P('fsdp', None, 'dp')
- new_right_stat: float32 [64, 1024, 1024], P('fsdp', None, 'dp')
- new_first: float32 [64, 1024, 1024], P('fsdp', None, 'dp')
- new_second: float32 [64, 1024, 1024], P('fsdp', None, 'dp')
- update: bfloat16 [4096, 8, 1024], P('fsdp', None, 'dp')
Inputs may be any that keep to these rules, and one draw needn't show every extreme that they name: `block_owner_index`: no fsdp index owns more than 2 blocks; a quarter of the fsdp indices own 2 blocks and a quarter own none.
All inputs are finite; a program needn't handle non-finite values.
Results may differ from a plain program's by a relative error of at most 0.013.
Values may be sent and summed in bfloat16 or wider, within the bound.
No kernel may reach another device: no remote copies, remote signals or barrier semaphores. Data moves between devices by JAX's collectives and lax.ppermute only.
A program may use at most 128 MiB of HBM per device.

v0:
```python
import jax
import jax.numpy as jnp
from jax import lax
from jax.sharding import PartitionSpec as P


def in_order(blocks, dim):
    blocks = jnp.moveaxis(blocks, 0, dim)
    dims = blocks.shape
    return blocks.reshape(*dims[:dim], dims[dim] * dims[dim + 1], *dims[dim + 2 :])


def on_gathered_pieces(array, axis, dim, work, out_dim):
    width = array.shape[dim]
    pieces = jnp.split(array, 2, axis=dim) if width % 2 == 0 else [array]
    initial = jnp.arange(lax.axis_size(axis)) * width
    blocks = [lax.all_gather(piece, axis) for piece in pieces]
    made = [jax.vmap(work)(b, initial + k * (width // len(pieces))) for k, b in enumerate(blocks)]
    return in_order(jnp.concatenate(made, axis=out_dim + 1), out_dim)


def slot_lookup_table(block_owner_index, block_grid_cell, slot_count, per_owner):
    block_ids = jnp.arange(block_owner_index.shape[0], dtype=jnp.int32)
    shared = (block_owner_index[:, None] == block_owner_index[None, :]) & (
        block_ids[None, :] < block_ids[:, None]
    )
    rank_in = jnp.sum(shared.astype(jnp.int32), axis=1)
    block_slot_index = block_owner_index * per_owner + rank_in
    slot_ids = jnp.arange(slot_count, dtype=jnp.int32)
    matches = (block_slot_index[None, :] == slot_ids[:, None]).astype(jnp.int32)
    filled_marker = jnp.sum(matches, axis=1)
    slot_grid_cell = jnp.sum(matches * block_grid_cell[None, :], axis=1)
    return (block_slot_index, filled_marker, slot_grid_cell)


def local(
    gradient,
    block_owner_index,
    block_grid_cell,
    left_eigen_basis,
    right_eigen_basis,
    left_statistic_matrix,
    right_statistic_matrix,
    first_adam_moment,
    second_adam_moment,
):
    replicas = lax.axis_size("dp")
    members = lax.axis_size("fsdp")
    member = lax.axis_index("fsdp")
    column_group = lax.axis_index("dp")
    per_owner = left_eigen_basis.shape[0]
    block = left_eigen_basis.shape[1]
    width = left_eigen_basis.shape[2]
    band_rows = gradient.shape[1]
    grid_cols = gradient.shape[2]
    bands = block // band_rows
    grid_rows = members // bands
    piece_rows = band_rows // members
    slot_count = per_owner * members
    partial_terms = gradient.reshape(band_rows, grid_cols, replicas, width).astype(jnp.float32)
    reduced = lax.psum_scatter(
        partial_terms.astype(jnp.bfloat16), "dp", scatter_dimension=2, tiled=True
    ).astype(jnp.float32)
    reduced = reduced.reshape(band_rows, grid_cols, width).astype(jnp.bfloat16)
    block_slot_index, filled_marker, slot_grid_cell = slot_lookup_table(
        block_owner_index, block_grid_cell, slot_count, per_owner
    )
    my_filled = lax.dynamic_slice_in_dim(filled_marker, member * per_owner, per_owner, 0)
    split_band = reduced.reshape(members, piece_rows, grid_cols, width)
    received = lax.all_to_all(split_band, "fsdp", split_axis=0, concat_axis=0, tiled=True)
    by_cell = received.reshape(grid_rows, bands, piece_rows, grid_cols, width)
    by_cell = jnp.transpose(by_cell, (0, 3, 1, 2, 4)).reshape(
        grid_rows * grid_cols, bands, piece_rows, width
    )
    leaving = jnp.take(by_cell, slot_grid_cell, axis=0)
    leaving = jnp.where((filled_marker > 0)[:, None, None, None], leaving, jnp.zeros_like(leaving))
    leaving = leaving.reshape(members, per_owner, bands, piece_rows, width)
    landed = lax.all_to_all(leaving, "fsdp", split_axis=0, concat_axis=0, tiled=True)
    col_piece = jnp.transpose(landed, (1, 2, 0, 3, 4)).reshape(per_owner, block, width)
    gathered = lax.all_gather(col_piece, "dp", axis=2, tiled=True)
    row_piece = lax.dynamic_slice_in_dim(gathered, column_group * width, width, 1)
    new_left = 0.95 * left_statistic_matrix + 0.05 * jnp.einsum(
        "sik,sjk->sij", gathered, row_piece, preferred_element_type=jnp.float32
    )
    new_right = 0.95 * right_statistic_matrix + 0.05 * jnp.einsum(
        "ski,skj->sij", gathered, col_piece, preferred_element_type=jnp.float32
    )
    half_turn = jnp.einsum("sik,sij->skj", left_eigen_basis, gathered.astype(jnp.float32)).astype(
        jnp.bfloat16
    )

    def turn_rows(piece, start):
        return jnp.einsum("skj,sjc->skc", piece.astype(jnp.float32), right_eigen_basis)

    turned = on_gathered_pieces(half_turn, "dp", 1, turn_rows, 1)
    new_first = 0.9 * first_adam_moment + 0.1 * turned
    new_second = 0.999 * second_adam_moment + 0.001 * turned * turned
    direction = new_first / (jnp.sqrt(new_second) + 1e-08)
    full_left = lax.all_gather(left_eigen_basis, "dp", axis=2, tiled=True)
    applied = jnp.einsum("sik,skc->sic", full_left, direction)
    piece = right_eigen_basis
    moved = lax.psum_scatter(
        jnp.einsum("sic,sjc->jsi", applied, piece), "dp", scatter_dimension=0, tiled=True
    )
    backward = jnp.transpose(moved.astype(jnp.bfloat16), (1, 2, 0))
    parted = backward.reshape(per_owner, bands, members, piece_rows, width)
    parted = jnp.transpose(parted, (2, 0, 1, 3, 4))
    parted = jnp.where((my_filled > 0)[None, :, None, None, None], parted, jnp.zeros_like(parted))
    homed = lax.all_to_all(parted, "fsdp", split_axis=0, concat_axis=0, tiled=True)
    homed = homed.reshape(slot_count, bands, piece_rows, width)
    all_cells = jnp.arange(grid_rows * grid_cols, dtype=jnp.int32)
    all_hits = (block_grid_cell[None, :] == all_cells[:, None]).astype(jnp.int32)
    cell_slot = jnp.sum(all_hits * block_slot_index[None, :], axis=1)
    per_cell = jnp.take(homed, cell_slot, axis=0).reshape(
        grid_rows, grid_cols, bands, piece_rows, width
    )
    per_cell = jnp.transpose(per_cell, (0, 2, 3, 1, 4)).reshape(
        members, piece_rows, grid_cols, width
    )
    update = lax.all_to_all(per_cell, "fsdp", split_axis=0, concat_axis=0, tiled=True).reshape(
        band_rows, grid_cols, width
    )
    return (new_left, new_right, new_first, new_second, update)


def solution(mesh):
    in_specs = (
        P("dp", "fsdp", None, None),
        P(),
        P(),
        P("fsdp", None, "dp"),
        P("fsdp", None, "dp"),
        P("fsdp", None, "dp"),
        P("fsdp", None, "dp"),
        P("fsdp", None, "dp"),
        P("fsdp", None, "dp"),
    )
    out_specs = (
        P("fsdp", None, "dp"),
        P("fsdp", None, "dp"),
        P("fsdp", None, "dp"),
        P("fsdp", None, "dp"),
        P("fsdp", None, "dp"),
    )
    return jax.shard_map(local, mesh=mesh, in_specs=in_specs, out_specs=out_specs, check_vma=False)
```

profile of v0, /device:TPU:1, one launch (start us, length us, event | category | flops | bytes accessed | tf_op | source)
XLA Modules:
  0.0 404.2 jit_solution(3661794692890048232)
XLA Ops:
  7.2 0.0 copy-start
  7.2 0.0 reduce-scatter.3.cloned.1.call-start
  7.2 3.2 copy.61
  10.4 0.0 reduce-scatter.3.cloned.1.call-update
  10.4 0.6 copy-done.6
  11.1 0.2 convert_reduce_fusion.1
  11.3 0.1 convert_reduce_fusion
  11.4 0.1 reduce_sum.47
  11.5 0.1 gt.22
  11.6 32.2 %reduce-scatter.3.cloned.1.call-done = bf16[128,8,1,256]{3,1,0,2:T(8,128)(2,1)} async-done(((bf16[128,8,4,256]{3,1,0,2:T(8,128)(2,1)}), bf16[128,8,1,256]{3,1,0,2:T(8,128)(2,1)}) %reduce-scatter.3.cloned.1.call-update) | async-done | bytes 524304 | tf_op jit(solution)/shard_map/reduce_scatter | solution.py:61
  43.8 7.8 %all-to-all-start = ((bf16[32,4,8,256]{3,2,1,0:T(8,128)(2,1)}), bf16[32,4,8,256]{3,2,1,0:T(8,128)(2,1)S(1)}, u32[]{:S(2)}, u32[]{:S(2)}) async-start(bf16[32,4,8,256]{3,2,1,0:T(8,128)(2,1)} %bitcast.89), calls=%async_computation.1 | async-start | bytes 1048576 | tf_op jit(solution)/shard_map/all_to_all | solution.py:70
  51.6 0.0 all-gather.7.cloned.1.call-start
  51.7 11.3 %all-to-all-done = bf16[32,4,8,256]{3,2,1,0:T(8,128)(2,1)S(1)} async-done(((bf16[32,4,8,256]{3,2,1,0:T(8,128)(2,1)}), bf16[32,4,8,256]{3,2,1,0:T(8,128)(2,1)S(1)}, u32[]{:S(2)}, u32[]{:S(2)}) %all-to-all-start) | async-done | bytes 524320 | tf_op jit(solution)/shard_map/all_to_all | solution.py:70
  63.0 0.3 copy.62
  63.3 1.6 gather_fusion
  64.9 1.4 select_select_fusion
  66.3 20.7 %all_to_all.20 = bf16[32,2,8,4,256]{4,2,3,1,0:T(8,128)(2,1)S(1)} all-to-all(bf16[32,2,8,4,256]{4,2,3,1,0:T(8,128)(2,1)S(1)} %select_select_fusion), channel_id=1, replica_groups=mesh['dp'=4,'fsdp'=32] {'fsdp'}, dimensions={0} | all-to-all | bytes 2097152 | tf_op jit(solution)/shard_map/all_to_all | solution.py:78
  87.0 0.5 copy.63
  87.5 1.1 reshape.101
  88.6 0.0 all-gather.7.cloned.1.call-update
  88.6 0.0 all-gather.13.cloned.1.call-start
  88.7 46.0 %all-gather.7.cloned.1.call-done = bf16[2,1024,1024]{2,1,0:T(8,128)(2,1)} async-done(((bf16[2,1024,256]{2,1,0:T(8,128)(2,1)}), bf16[2,1024,1024]{2,1,0:T(8,128)(2,1)}) %all-gather.7.cloned.1.call-update) | async-done | bytes 4194320 | tf_op jit(solution)/shard_map/all_gather | solution.py:80
  134.7 4.6 %fusion.16 = bf16[2,256,1024]{1,2,0:T(8,128)(2,1)S(1)} fusion(bf16[2,1024,1024]{2,1,0:T(8,128)(2,1)} %all-gather.7.cloned.1.call-done, f32[2,1024,256]{2,1,0:T(8,128)} %param.12), kind=kOutput, calls=%fused_computation.21 | convolution fusion | flops 1073741824 | bytes 7340032 | tf_op jit(solution)/shard_map/sik,sij->skj/dot_general | solution.py:88
  139.3 0.2 fusion.39
  139.5 1.0 copy.68
  140.5 0.0 all-gather.13.cloned.1.call-update
  140.5 0.0 all-gather.11.cloned.1.call-start
  140.6 1.0 copy.66
  141.6 0.0 all-gather.11.cloned.1.call-update
  141.6 0.0 all-gather.9.cloned.1.call-start
  141.6 2.7 convert.4
  144.3 0.0 all-gather.9.cloned.1.call-update
  144.3 0.0 reduce-scatter.5.cloned.1.call-start
  144.4 29.2 %all-gather.13.cloned.1.call-done = bf16[8,128,1024]{2,1,0:T(8,128)(2,1)} async-done(((bf16[2,128,1024]{2,1,0:T(8,128)(2,1)}), bf16[8,128,1024]{2,1,0:T(8,128)(2,1)}) %all-gather.13.cloned.1.call-update) | async-done | bytes 2097168 | tf_op jit(solution)/shard_map/all_gather | solution.py:17
  173.6 2.3 fusion.22
  175.9 30.6 %all-gather.11.cloned.1.call-done = bf16[8,128,1024]{2,1,0:T(8,128)(2,1)} async-done(((bf16[2,128,1024]{2,1,0:T(8,128)(2,1)}), bf16[8,128,1024]{2,1,0:T(8,128)(2,1)}) %all-gather.11.cloned.1.call-update) | async-done | bytes 2097168 | tf_op jit(solution)/shard_map/all_gather | solution.py:17
  206.5 2.3 fusion.17
  208.8 0.0 copy-start.3
  208.8 0.0 copy-start.4
  208.8 0.1 pad_maximum_fusion
  208.9 1.4 copy-done.3
  210.4 0.6 copy-done.4
  211.0 2.6 fusion
  213.6 45.1 %all-gather.9.cloned.1.call-done = bf16[2,1024,1024]{2,1,0:T(8,128)(2,1)} async-done(((bf16[2,1024,256]{2,1,0:T(8,128)(2,1)}), bf16[2,1024,1024]{2,1,0:T(8,128)(2,1)}) %all-gather.9.cloned.1.call-update) | async-done | bytes 4194320 | tf_op jit(solution)/shard_map/all_gather | solution.py:99
  258.7 9.2 %convolution_bitcast_fusion = f32[1024,2,1024]{0,2,1:T(8,128)} fusion(f32[2,1024,256]{2,1,0:T(8,128)S(1)} %copy-done, bf16[2,1024,1024]{2,1,0:T(8,128)(2,1)} %all-gather.9.cloned.1.call-done, f32[2,1024,256]{2,1,0:T(8,128)} %get-tuple-element.18, f32[2,1024,256]{2,1,0:T(8,128)} %get-tuple-element.19), kind=kOutput, calls=%fused_computation.2 | convolution fusion | flops 2148532224 | bytes 18874368 | tf_op jit(solution)/shard_map/sic,sjc->jsi/dot_general | solution.py:103
  267.9 0.0 reduce-scatter.5.cloned.1.call-update
  268.0 0.1 select_reduce_fusion
  268.1 0.1 reduce_sum.50
  268.2 0.1 dynamic-slice_compare_fusion
  268.2 82.6 %reduce-scatter.5.cloned.1.call-done = f32[256,2,1024]{0,2,1:T(8,128)} async-done(((f32[1024,2,1024]{0,2,1:T(8,128)}), f32[256,2,1024]{0,2,1:T(8,128)}) %reduce-scatter.5.cloned.1.call-update) | async-done | bytes 2097168 | tf_op jit(solution)/shard_map/reduce_scatter | solution.py:102
  350.9 1.7 convert_bitcast_fusion
  352.6 0.3 reshape.103
  352.9 0.0 copy-start.2
  352.9 1.6 fusion.27
  354.5 7.8 %all-to-all-start.2 = ((bf16[32,2,8,4,256]{4,2,3,1,0:T(8,128)(2,1)}), bf16[32,2,8,4,256]{4,2,3,1,0:T(8,128)(2,1)S(1)}, u32[]{:S(2)}, u32[]{:S(2)}) async-start(bf16[32,2,8,4,256]{4,2,3,1,0:T(8,128)(2,1)} %fusion.27), calls=%async_computation.4 | async-start | bytes 2097152 | tf_op jit(solution)/shard_map/all_to_all | solution.py:109
  362.3 5.9 %multiply_add_fusion = f32[2,1024,256]{2,1,0:T(8,128)} fusion(f32[2,1024,256]{2,1,0:T(8,128)} %param.15, bf16[2,1024,1024]{2,1,0:T(8,128)(2,1)} %all-gather.7.cloned.1.call-done, bf16[2,1024,256]{2,1,0:T(8,128)(2,1)S(1)} %copy-done.2), kind=kOutput, calls=%fused_computation.18 | convolution fusion | flops 1075314688 | bytes 9437184 | tf_op jit(solution)/shard_map/ski,skj->sij/dot_general | solution.py:85
  368.2 11.1 %all-to-all-done.2 = bf16[32,2,8,4,256]{4,2,3,1,0:T(8,128)(2,1)S(1)} async-done(((bf16[32,2,8,4,256]{4,2,3,1,0:T(8,128)(2,1)}), bf16[32,2,8,4,256]{4,2,3,1,0:T(8,128)(2,1)S(1)}, u32[]{:S(2)}, u32[]{:S(2)}) %all-to-all-start.2) | async-done | bytes 1048608 | tf_op jit(solution)/shard_map/all_to_all | solution.py:109
  379.3 0.6 gather_fusion.1
  379.9 0.1 select_bitcast_fusion
  380.0 1.1 copy.73
  381.1 3.9 all-to-all-start.3
  385.0 6.0 %multiply_add_fusion.1 = f32[2,1024,256]{2,1,0:T(8,128)} fusion(f32[2,1024,256]{2,1,0:T(8,128)} %param.14, bf16[2,1024,1024]{2,1,0:T(8,128)(2,1)} %all-gather.7.cloned.1.call-done, s32[]{:T(128)S(6)} %select_n.66), kind=kOutput, calls=%fused_computation.19 | convolution fusion | flops 1075314688 | bytes 9437188 | tf_op jit(solution)/shard_map/sik,sjk->sij/dot_general | solution.py:82
  391.0 5.5 %all-to-all-done.3 = bf16[32,4,8,256]{3,2,1,0:T(8,128)(2,1)S(1)} async-done(((bf16[32,4,8,256]{3,2,1,0:T(8,128)(2,1)}), bf16[32,4,8,256]{3,2,1,0:T(8,128)(2,1)S(1)}, u32[]{:S(2)}, u32[]{:S(2)}) %all-to-all-start.3) | async-done | bytes 524320 | tf_op jit(solution)/shard_map/all_to_all | solution.py:120
  396.6 0.8 copy.91
  (15 shorter events, 0.1 us)
Async XLA Ops:
  7.2 166.4 %copy-start = (f32[2,1024,256]{2,1,0:T(8,128)S(1)}, f32[2,1024,256]{2,1,0:T(8,128)}, u32[]{:S(2)}) copy-start(f32[2,1024,256]{2,1,0:T(8,128)} %param.13) | copy-start | bytes 6291460
  7.2 36.6 %reduce-scatter.3.cloned.1.call-start = ((), (), s32[]{:S(2)}) async-start(), calls=%async_computation.6 | async-start | bytes 2621440 | tf_op jit(solution)/shard_map/reduce_scatter | solution.py:61
  10.4 0.7 copy-start.6
  10.4 0.8 copy-start.5
  43.8 19.2 %all-to-all-start = ((bf16[32,4,8,256]{3,2,1,0:T(8,128)(2,1)}), bf16[32,4,8,256]{3,2,1,0:T(8,128)(2,1)S(1)}, u32[]{:S(2)}, u32[]{:S(2)}) async-start(bf16[32,4,8,256]{3,2,1,0:T(8,128)(2,1)} %bitcast.89), calls=%async_computation.1 | async-start | bytes 1048576 | tf_op jit(solution)/shard_map/all_to_all | solution.py:70
  51.6 83.1 %all-gather.7.cloned.1.call-start = ((), (), s32[]{:S(2)}) async-start(), calls=%async_computation.7 | async-start | bytes 5242880 | tf_op jit(solution)/shard_map/all_gather | solution.py:80
  88.6 84.9 %all-gather.13.cloned.1.call-start = ((), (), s32[]{:S(2)}) async-start(), calls=%async_computation.11 | async-start | bytes 2621440 | tf_op jit(solution)/shard_map/all_gather | solution.py:17
  140.5 66.0 %all-gather.11.cloned.1.call-start = ((), (), s32[]{:S(2)}) async-start(), calls=%async_computation.10 | async-start | bytes 2621440 | tf_op jit(solution)/shard_map/all_gather | solution.py:17
  141.6 117.2 %all-gather.9.cloned.1.call-start = ((), (), s32[]{:S(2)}) async-start(), calls=%async_computation.8 | async-start | bytes 5242880 | tf_op jit(solution)/shard_map/all_gather | solution.py:99
  144.3 206.5 %reduce-scatter.5.cloned.1.call-start = ((), (), s32[]{:S(2)}) async-start(), calls=%async_computation.9 | async-start | bytes 10485760 | tf_op jit(solution)/shard_map/reduce_scatter | solution.py:102
  208.8 1.6 copy-start.3
  208.8 2.2 copy-start.4
  352.9 9.4 %copy-start.2 = (bf16[2,1024,256]{2,1,0:T(8,128)(2,1)S(1)}, bf16[2,1024,256]{2,1,0:T(8,128)(2,1)}, u32[]{:S(2)}) copy-start(bf16[2,1024,256]{2,1,0:T(8,128)(2,1)} %reshape.101) | copy-start | bytes 3145732
  354.5 24.8 %all-to-all-start.2 = ((bf16[32,2,8,4,256]{4,2,3,1,0:T(8,128)(2,1)}), bf16[32,2,8,4,256]{4,2,3,1,0:T(8,128)(2,1)S(1)}, u32[]{:S(2)}, u32[]{:S(2)}) async-start(bf16[32,2,8,4,256]{4,2,3,1,0:T(8,128)(2,1)} %fusion.27), calls=%async_computation.4 | async-start | bytes 2097152 | tf_op jit(solution)/shard_map/all_to_all | solution.py:109
  381.1 15.5 %all-to-all-start.3 = ((bf16[32,4,8,256]{3,2,1,0:T(8,128)(2,1)}), bf16[32,4,8,256]{3,2,1,0:T(8,128)(2,1)S(1)}, u32[]{:S(2)}, u32[]{:S(2)}) async-start(bf16[32,4,8,256]{3,2,1,0:T(8,128)(2,1)} %bitcast.28), calls=%async_computation.5 | async-start | bytes 1048576 | tf_op jit(solution)/shard_map/all_to_all | solution.py:120
  385.0 12.3 %copy-start.1 = (f32[2,1024,256]{2,1,0:T(8,128)S(1)}, f32[2,1024,256]{2,1,0:T(8,128)}, u32[]{:S(2)}) copy-start(f32[2,1024,256]{2,1,0:T(8,128)} %param.13) | copy-start | bytes 6291460
Sparse Core Ops, SparseCore 0:
  11.0 32.7 reduce-scatter.2
  88.8 45.8 all-gather.6
  140.6 32.8 all-gather.12
  175.6 30.7 all-gather.10
  208.5 50.1 all-gather.8
  268.1 82.7 reduce-scatter.4
where the time goes:
time: 405 us; the launch traced here: 404 us
  waiting for transfers between devices  294 us (73%)
  matrix products  30.3 us (7%)
  blocking collectives  20.7 us (5%)
  starting transfers between devices  19.7 us (5%)
  local copies, waits for them, and re-layouts  14.6 us (4%)
  between operations  14.3 us (4%)
  other arithmetic  10.8 us (3%)
    reduce_scatter x1, waiting for transfers between devices, local(): lax.psum_scatter(jnp.einsum('sic,sjc->jsi', applied, piece), 'dp', scatte...  82.6 us
    all_gather x2, waiting for transfers between devices, on_gathered_pieces(): blocks = [lax.all_gather(piece, axis) for piece in pieces]  59.8 us
    all_gather x1, waiting for transfers between devices, local(): gathered = lax.all_gather(col_piece, 'dp', axis=2, tiled=True)  46 us
    all_gather x1, waiting for transfers between devices, local(): full_left = lax.all_gather(left_eigen_basis, 'dp', axis=2, tiled=True)  45.1 us
    reduce_scatter x1, waiting for transfers between devices, local(): lax.psum_scatter(partial_terms.astype(jnp.bfloat16), 'dp', scatter_dimens...  32.2 us
    all_to_all x1, blocking collectives, local(): lax.all_to_all(leaving, 'fsdp', split_axis=0, concat_axis=0, tiled=True)  20.7 us
    all_to_all x1, waiting for transfers between devices, local(): lax.all_to_all(split_band, 'fsdp', split_axis=0, concat_axis=0, tiled=True)  11.3 us
    all_to_all x1, waiting for transfers between devices, local(): lax.all_to_all(parted, 'fsdp', split_axis=0, concat_axis=0, tiled=True)  11.1 us
  transfers between devices with their start and end apart: 9, of which 9 were waited for; matrix products, arithmetic and copies ran while one was open for 6% of the time, Pallas kernels for 0%

commit v1 on v0

--- a/solution.py
+++ b/solution.py
@@ -2,6 +2,11 @@
 import jax.numpy as jnp
 from jax import lax
 from jax.sharding import PartitionSpec as P
+
+
+def all_parts(value, axis, dim):
+    blocks = lax.all_gather(value, axis)
+    return jnp.concatenate(blocks, axis=dim)
 
 
 def in_order(blocks, dim):
@@ -77,7 +82,7 @@
     leaving = leaving.reshape(members, per_owner, bands, piece_rows, width)
     landed = lax.all_to_all(leaving, "fsdp", split_axis=0, concat_axis=0, tiled=True)
     col_piece = jnp.transpose(landed, (1, 2, 0, 3, 4)).reshape(per_owner, block, width)
-    gathered = lax.all_gather(col_piece, "dp", axis=2, tiled=True)
+    gathered = all_parts(col_piece, "dp", 2)
     row_piece = lax.dynamic_slice_in_dim(gathered, column_group * width, width, 1)
     new_left = 0.95 * left_statistic_matrix + 0.05 * jnp.einsum(
         "sik,sjk->sij", gathered, row_piece, preferred_element_type=jnp.float32

time: 405 us -> 405 us (level)
  local copies, waits for them, and re-layouts: 14.6 us -> 23.3 us
  waiting for transfers between devices: 294 us -> 287 us
  transfers between devices with their start and end apart: 9 -> 9, of which waited for: 9 -> 9; matrix products, arithmetic and copies ran while one was open for 6% -> 7% of each run, Pallas kernels for 0% -> 0%
where the time goes in v1:
time: 405 us
  waiting for transfers between devices  287 us (71%)
  matrix products  28.6 us (7%)
  local copies, waits for them, and re-layouts  23.3 us (6%)
  blocking collectives  20.7 us (5%)
  starting transfers between devices  20 us (5%)
  between operations  14.4 us (4%)
  other arithmetic  10.8 us (3%)
    reduce_scatter x1, waiting for transfers between devices, local(): lax.psum_scatter(jnp.einsum('sic,sjc->jsi', applied, piece), 'dp', scatte...  82.6 us
    all_gather x2, waiting for transfers between devices, on_gathered_pieces(): blocks = [lax.all_gather(piece, axis) for piece in pieces]  55.8 us
    all_gather x1, waiting for transfers between devices, local(): full_left = lax.all_gather(left_eigen_basis, 'dp', axis=2, tiled=True)  45 us
    all_gather x1, waiting for transfers between devices, all_parts(): blocks = lax.all_gather(value, axis)  44 us
    reduce_scatter x1, waiting for transfers between devices, local(): lax.psum_scatter(partial_terms.astype(jnp.bfloat16), 'dp', scatter_dimens...  32.2 us
    all_to_all x1, blocking collectives, local(): lax.all_to_all(leaving, 'fsdp', split_axis=0, concat_axis=0, tiled=True)  20.7 us
    all_to_all x1, waiting for transfers between devices, local(): lax.all_to_all(split_band, 'fsdp', split_axis=0, concat_axis=0, tiled=True)  11.3 us
    all_to_all x1, waiting for transfers between devices, local(): lax.all_to_all(parted, 'fsdp', split_axis=0, concat_axis=0, tiled=True)  10.3 us
  transfers between devices with their start and end apart: 9, of which 9 were waited for; matrix products, arithmetic and copies ran while one was open for 7% of the time, Pallas kernels for 0%

profile of v1, /device:TPU:1, one launch (start us, length us, event | category | flops | bytes accessed | tf_op | source)
XLA Modules:
  0.0 404.6 jit_solution(3515564762040194707)
XLA Ops:
  7.2 0.0 reduce-scatter.3.cloned.1.call-start
  7.2 3.2 copy.71
  10.4 0.0 reduce-scatter.3.cloned.1.call-update
  10.4 0.6 copy-done.8
  11.1 0.2 convert_reduce_fusion.1
  11.3 0.1 convert_reduce_fusion
  11.4 0.1 reduce_sum.47
  11.5 0.1 gt.22
  11.6 32.2 %reduce-scatter.3.cloned.1.call-done = bf16[128,8,1,256]{3,1,0,2:T(8,128)(2,1)} async-done(((bf16[128,8,4,256]{3,1,0,2:T(8,128)(2,1)}), bf16[128,8,1,256]{3,1,0,2:T(8,128)(2,1)}) %reduce-scatter.3.cloned.1.call-update) | async-done | bytes 524304 | tf_op jit(solution)/shard_map/reduce_scatter | solution.py:66
  43.8 7.8 %all-to-all-start = ((bf16[32,4,8,256]{3,2,1,0:T(8,128)(2,1)}), bf16[32,4,8,256]{3,2,1,0:T(8,128)(2,1)S(1)}, u32[]{:S(2)}, u32[]{:S(2)}) async-start(bf16[32,4,8,256]{3,2,1,0:T(8,128)(2,1)} %bitcast.98), calls=%async_computation.1 | async-start | bytes 1048576 | tf_op jit(solution)/shard_map/all_to_all | solution.py:75
  51.6 0.0 all-gather.7.cloned.1.call-start
  51.7 11.3 %all-to-all-done = bf16[32,4,8,256]{3,2,1,0:T(8,128)(2,1)S(1)} async-done(((bf16[32,4,8,256]{3,2,1,0:T(8,128)(2,1)}), bf16[32,4,8,256]{3,2,1,0:T(8,128)(2,1)S(1)}, u32[]{:S(2)}, u32[]{:S(2)}) %all-to-all-start) | async-done | bytes 524320 | tf_op jit(solution)/shard_map/all_to_all | solution.py:75
  63.0 0.3 copy.72
  63.3 1.6 gather_fusion
  64.9 1.4 select_select_fusion
  66.3 20.7 %all_to_all.20 = bf16[32,2,8,4,256]{4,2,3,1,0:T(8,128)(2,1)S(1)} all-to-all(bf16[32,2,8,4,256]{4,2,3,1,0:T(8,128)(2,1)S(1)} %select_select_fusion), channel_id=1, replica_groups=mesh['dp'=4,'fsdp'=32] {'fsdp'}, dimensions={0} | all-to-all | bytes 2097152 | tf_op jit(solution)/shard_map/all_to_all | solution.py:83
  87.0 1.1 copy.73
  88.1 1.1 copy.74
  89.2 0.0 all-gather.7.cloned.1.call-update
  89.2 0.0 all-gather.13.cloned.1.call-start
  89.3 44.0 %all-gather.7.cloned.1.call-done = bf16[4,2,1024,256]{3,2,1,0:T(8,128)(2,1)} async-done(((bf16[1,2,1024,256]{3,2,1,0:T(8,128)(2,1)}), bf16[4,2,1024,256]{3,2,1,0:T(8,128)(2,1)}) %all-gather.7.cloned.1.call-update) | async-done | bytes 4194320 | tf_op jit(solution)/shard_map/all_gather | solution.py:8
  133.3 2.9 copy.92
  136.2 1.8 fusion.16
  138.0 0.1 copy-done.2
  138.2 1.1 fusion.39
  139.3 2.0 copy.81
  141.4 0.0 all-gather.13.cloned.1.call-update
  141.4 0.0 all-gather.11.cloned.1.call-start
  141.4 2.0 copy.79
  143.5 0.0 all-gather.11.cloned.1.call-update
  143.5 0.0 all-gather.9.cloned.1.call-start
  143.6 2.7 convert.4
  146.2 0.0 all-gather.9.cloned.1.call-update
  146.2 0.2 reduce-scatter.5.cloned.1.call-start
  146.5 26.2 %all-gather.13.cloned.1.call-done = bf16[8,128,1024]{2,1,0:T(8,128)(2,1)} async-done(((bf16[2,128,1024]{2,1,0:T(8,128)(2,1)}), bf16[8,128,1024]{2,1,0:T(8,128)(2,1)}) %all-gather.13.cloned.1.call-update) | async-done | bytes 2097168 | tf_op jit(solution)/shard_map/all_gather | solution.py:22
  172.6 3.3 fusion.22
  175.9 29.6 %all-gather.11.cloned.1.call-done = bf16[8,128,1024]{2,1,0:T(8,128)(2,1)} async-done(((bf16[2,128,1024]{2,1,0:T(8,128)(2,1)}), bf16[8,128,1024]{2,1,0:T(8,128)(2,1)}) %all-gather.11.cloned.1.call-update) | async-done | bytes 2097168 | tf_op jit(solution)/shard_map/all_gather | solution.py:22
  205.5 2.4 fusion.17
  208.0 0.1 pad_maximum_fusion
  208.1 1.4 copy-done.5
  209.5 0.6 copy-done.6
  210.2 2.6 fusion
  212.8 45.0 %all-gather.9.cloned.1.call-done = bf16[2,1024,1024]{2,1,0:T(8,128)(2,1)} async-done(((bf16[2,1024,256]{2,1,0:T(8,128)(2,1)}), bf16[2,1024,1024]{2,1,0:T(8,128)(2,1)}) %all-gather.9.cloned.1.call-update) | async-done | bytes 4194320 | tf_op jit(solution)/shard_map/all_gather | solution.py:104
  257.8 9.2 %convolution_bitcast_fusion = f32[1024,2,1024]{0,2,1:T(8,128)} fusion(f32[2,1024,256]{2,1,0:T(8,128)S(1)} %copy-done, bf16[2,1024,1024]{2,1,0:T(8,128)(2,1)} %all-gather.9.cloned.1.call-done, f32[2,1024,256]{2,1,0:T(8,128)} %get-tuple-element.18, f32[2,1024,256]{2,1,0:T(8,128)} %get-tuple-element.19), kind=kOutput, calls=%fused_computation.2 | convolution fusion | flops 2148532224 | bytes 18874368 | tf_op jit(solution)/shard_map/sic,sjc->jsi/dot_general | solution.py:108
  267.0 0.0 reduce-scatter.5.cloned.1.call-update
  267.0 0.1 select_reduce_fusion
  267.2 0.1 reduce_sum.50
  267.2 0.1 dynamic-slice_compare_fusion
  267.3 82.6 %reduce-scatter.5.cloned.1.call-done = f32[256,2,1024]{0,2,1:T(8,128)} async-done(((f32[1024,2,1024]{0,2,1:T(8,128)}), f32[256,2,1024]{0,2,1:T(8,128)}) %reduce-scatter.5.cloned.1.call-update) | async-done | bytes 2097168 | tf_op jit(solution)/shard_map/reduce_scatter | solution.py:107
  350.0 1.7 convert_bitcast_fusion
  351.7 0.3 reshape.111
  351.9 1.6 fusion.27
  353.5 7.8 %all-to-all-start.2 = ((bf16[32,2,8,4,256]{4,2,3,1,0:T(8,128)(2,1)}), bf16[32,2,8,4,256]{4,2,3,1,0:T(8,128)(2,1)}, u32[]{:S(2)}, u32[]{:S(2)}) async-start(bf16[32,2,8,4,256]{4,2,3,1,0:T(8,128)(2,1)} %fusion.27), calls=%async_computation.4 | async-start | bytes 2097152 | tf_op jit(solution)/shard_map/all_to_all | solution.py:114
  361.4 0.5 copy.76
  361.9 0.3 reshape.109
  362.2 5.9 %multiply_add_fusion = f32[2,1024,256]{2,1,0:T(8,128)} fusion(f32[2,1024,256]{2,1,0:T(8,128)} %param.15, bf16[2,1024,1024]{2,1,0:T(8,128)(2,1)} %bitcast.84, bf16[2,1024,256]{2,1,0:T(8,128)(2,1)S(1)} %reshape.109), kind=kOutput, calls=%fused_computation.18 | convolution fusion | flops 1075314688 | bytes 9437184 | tf_op jit(solution)/shard_map/ski,skj->sij/dot_general | solution.py:90
  368.1 10.3 %all-to-all-done.2 = bf16[32,2,8,4,256]{4,2,3,1,0:T(8,128)(2,1)} async-done(((bf16[32,2,8,4,256]{4,2,3,1,0:T(8,128)(2,1)}), bf16[32,2,8,4,256]{4,2,3,1,0:T(8,128)(2,1)}, u32[]{:S(2)}, u32[]{:S(2)}) %all-to-all-start.2) | async-done | bytes 1048608 | tf_op jit(solution)/shard_map/all_to_all | solution.py:114
  378.4 1.8 gather_fusion.1
  380.3 0.1 select_bitcast_fusion
  380.4 1.1 copy.86
  381.5 3.9 all-to-all-start.3
  385.4 6.0 %multiply_add_fusion.1 = f32[2,1024,256]{2,1,0:T(8,128)} fusion(f32[2,1024,256]{2,1,0:T(8,128)} %param.14, bf16[2,1024,1024]{2,1,0:T(8,128)(2,1)} %bitcast.85, s32[]{:T(128)S(6)} %select_n.66), kind=kOutput, calls=%fused_computation.19 | convolution fusion | flops 1075314688 | bytes 9437188 | tf_op jit(solution)/shard_map/sik,sjk->sij/dot_general | solution.py:87
  391.4 5.5 %all-to-all-done.3 = bf16[32,4,8,256]{3,2,1,0:T(8,128)(2,1)S(1)} async-done(((bf16[32,4,8,256]{3,2,1,0:T(8,128)(2,1)}), bf16[32,4,8,256]{3,2,1,0:T(8,128)(2,1)S(1)}, u32[]{:S(2)}, u32[]{:S(2)}) %all-to-all-start.3) | async-done | bytes 524320 | tf_op jit(solution)/shard_map/all_to_all | solution.py:125
  397.0 0.8 copy.105
  (22 shorter events, 0.1 us)
Async XLA Ops:
  7.2 165.5 %copy-start = (f32[2,1024,256]{2,1,0:T(8,128)S(1)}, f32[2,1024,256]{2,1,0:T(8,128)}, u32[]{:S(2)}) copy-start(f32[2,1024,256]{2,1,0:T(8,128)} %param.13) | copy-start | bytes 6291460
  7.2 36.6 %reduce-scatter.3.cloned.1.call-start = ((), (), s32[]{:S(2)}) async-start(), calls=%async_computation.6 | async-start | bytes 2621440 | tf_op jit(solution)/shard_map/reduce_scatter | solution.py:66
  10.4 0.7 copy-start.8
  10.4 0.8 copy-start.7
  43.8 19.2 %all-to-all-start = ((bf16[32,4,8,256]{3,2,1,0:T(8,128)(2,1)}), bf16[32,4,8,256]{3,2,1,0:T(8,128)(2,1)S(1)}, u32[]{:S(2)}, u32[]{:S(2)}) async-start(bf16[32,4,8,256]{3,2,1,0:T(8,128)(2,1)} %bitcast.98), calls=%async_computation.1 | async-start | bytes 1048576 | tf_op jit(solution)/shard_map/all_to_all | solution.py:75
  51.6 81.7 %all-gather.7.cloned.1.call-start = ((), (), s32[]{:S(2)}) async-start(), calls=%async_computation.7 | async-start | bytes 5242880 | tf_op jit(solution)/shard_map/all_gather | solution.py:8
  89.2 83.4 %all-gather.13.cloned.1.call-start = ((), (), s32[]{:S(2)}) async-start(), calls=%async_computation.11 | async-start | bytes 2621440 | tf_op jit(solution)/shard_map/all_gather | solution.py:22
  133.3 2.9 copy-start.3
  136.2 2.0 copy-start.2
  141.4 64.1 %all-gather.11.cloned.1.call-start = ((), (), s32[]{:S(2)}) async-start(), calls=%async_computation.10 | async-start | bytes 2621440 | tf_op jit(solution)/shard_map/all_gather | solution.py:22
  143.5 114.3 %all-gather.9.cloned.1.call-start = ((), (), s32[]{:S(2)}) async-start(), calls=%async_computation.8 | async-start | bytes 5242880 | tf_op jit(solution)/shard_map/all_gather | solution.py:104
  146.2 203.7 %reduce-scatter.5.cloned.1.call-start = ((), (), s32[]{:S(2)}) async-start(), calls=%async_computation.9 | async-start | bytes 10485760 | tf_op jit(solution)/shard_map/reduce_scatter | solution.py:107
  205.5 2.4 copy-start.4
  207.9 1.6 copy-start.5
  207.9 2.2 copy-start.6
  353.5 24.9 %all-to-all-start.2 = ((bf16[32,2,8,4,256]{4,2,3,1,0:T(8,128)(2,1)}), bf16[32,2,8,4,256]{4,2,3,1,0:T(8,128)(2,1)}, u32[]{:S(2)}, u32[]{:S(2)}) async-start(bf16[32,2,8,4,256]{4,2,3,1,0:T(8,128)(2,1)} %fusion.27), calls=%async_computation.4 | async-start | bytes 2097152 | tf_op jit(solution)/shard_map/all_to_all | solution.py:114
  381.5 15.5 %all-to-all-start.3 = ((bf16[32,4,8,256]{3,2,1,0:T(8,128)(2,1)}), bf16[32,4,8,256]{3,2,1,0:T(8,128)(2,1)S(1)}, u32[]{:S(2)}, u32[]{:S(2)}) async-start(bf16[32,4,8,256]{3,2,1,0:T(8,128)(2,1)} %bitcast.30), calls=%async_computation.5 | async-start | bytes 1048576 | tf_op jit(solution)/shard_map/all_to_all | solution.py:125
  385.4 12.3 %copy-start.1 = (f32[2,1024,256]{2,1,0:T(8,128)S(1)}, f32[2,1024,256]{2,1,0:T(8,128)}, u32[]{:S(2)}) copy-start(f32[2,1024,256]{2,1,0:T(8,128)} %param.13) | copy-start | bytes 6291460
Sparse Core Ops, SparseCore 0:
  11.0 32.7 reduce-scatter.2
  89.3 43.8 all-gather.6
  141.5 31.0 all-gather.12
  174.7 30.7 all-gather.10
  207.6 50.1 all-gather.8
  267.2 82.7 reduce-scatter.4
